TPU v7x, 32 devices: a whole 2x2x4 slice. The times are simulated.
32 devices in a mesh: section: 2 (over core), dp: 16 (over z, y, x).
Axes of the slice: x: 2, y: 2, z: 4, core: 2. Of those that a mesh axis runs over, the one named last changes fastest.
Arguments:
- replay: bfloat16 [2048, 4096], P('dp'), may hold values from -6 to 6
- state_ids: int32 [2048], P('dp'), may hold values from 0 to 2047, as said below
- sampled: int32 [2048, 20], P('dp'), may hold values from 0 to 255
- targets: int32 [2048], P('dp'), may hold values from 0 to 19
- action_table: bfloat16 [256, 4096], replicated, may hold values from -6 to 6
- norm_gain: float32 [2, 4096], P('section'), may hold values from 0.5 to 1.5
- w_up: bfloat16 [2, 4096, 512], P('section', 'dp'), may hold values from -0.09375 to 0.09375
- w_down: bfloat16 [2, 512, 4096], P('section', 'dp'), may hold values from -0.25 to 0.25
Outputs:
- grad_up: float32 [2, 4096, 512], P('section', 'dp')
- grad_down: float32 [2, 512, 4096], P('section', 'dp')
- grad_gain: float32 [2, 4096], P('section')
- loss: float32 [], replicated
Inputs may be any that keep to these rules, and one draw needn't show every extreme that they name: state_ids[i] // 128 == i // 128: a state's replay row lies in the same aligned block of 128 rows as the state.
All inputs are finite; a program needn't handle non-finite values.
Results may differ from a plain program's by a relative error of at most 0.011.
Values may be sent and summed in bfloat16 or wider, within the bound.
A program may use at most 128 MiB of HBM per device.

v0:
```python
import math

import jax
import jax.numpy as jnp
from jax import lax
from jax.sharding import PartitionSpec as P

ROWS_DEV = 128


epsilon = 1e-06
logit_cap = 15.0


def passed_along(value, axis, by):
    peers = lax.axis_size(axis)
    pairs = [(i, i + by) for i in range(peers) if 0 <= i + by < peers]
    return lax.ppermute(value, axis, pairs)


def contract_last(left, right):
    return lax.dot_general(
        left, right, (((1,), (1,)), ((), ())), preferred_element_type=jnp.float32
    )


def contract_first(left, right):
    return lax.dot_general(
        left, right, (((0,), (0,)), ((), ())), preferred_element_type=jnp.float32
    )


def layer_forward(states, gain_row, up_proj, down_proj):
    wide = states.astype(jnp.float32)
    recip = lax.rsqrt(jnp.mean(wide * wide, -1, keepdims=True) + epsilon)
    normed = (wide * recip * gain_row).astype(jnp.bfloat16)
    upper = jnp.dot(normed, up_proj, preferred_element_type=jnp.float32)
    sigm = jax.nn.sigmoid(upper)
    active = (upper * sigm).astype(jnp.bfloat16)
    result = (wide + jnp.dot(active, down_proj, preferred_element_type=jnp.float32)).astype(
        jnp.bfloat16
    )
    return (result, (wide, recip, normed, upper, sigm, active))


def layer_backward(grad_out, cache, gain_row, up_proj, down_proj):
    wide, recip, normed, upper, sigm, active = cache
    grad_act = contract_last(grad_out, down_proj)
    grad_upper = (grad_act * sigm * (1.0 + upper * (1.0 - sigm))).astype(jnp.bfloat16)
    grad_norm = contract_last(grad_upper, up_proj)
    scaled = grad_norm * gain_row
    gain_term = jnp.sum(grad_norm * wide * recip, 0)
    grad_in = (
        grad_out.astype(jnp.float32)
        + scaled * recip
        - wide * recip**3 * jnp.mean(scaled * wide, -1, keepdims=True)
    )
    return (grad_in.astype(jnp.bfloat16), grad_upper, gain_term)


def head_tail(chosen, targets, scale):
    bent = jnp.tanh(chosen / logit_cap)
    logits = logit_cap * bent
    expo = jnp.exp(logits)
    summed = jnp.sum(expo, -1, keepdims=True)
    target_hot = (targets[:, None] == jnp.arange(chosen.shape[1])[None, :]).astype(jnp.float32)
    cross = jnp.log(summed[:, 0]) - jnp.sum(logits * target_hot, -1)
    loss_sum = jnp.sum(cross) / ROWS_DEV
    d_logits = (expo / summed - target_hot) / ROWS_DEV
    d_chosen = d_logits * (1.0 - bent * bent) / scale
    return (loss_sum, d_chosen)


def store_block(buffer, block_pos, value, keep):
    current = lax.dynamic_index_in_dim(buffer, block_pos, 0, keepdims=False)
    return lax.dynamic_update_index_in_dim(buffer, jnp.where(keep, value, current), block_pos, 0)


def on_device(replay, state_ids, sampled, targets, action_table, norm_gain, w_up, w_down):
    section_pos = lax.axis_index("section")
    section_count = lax.axis_size("section")
    final_section = section_count - 1
    up_proj, down_proj = (
        lax.all_gather(w_up[0], "dp", axis=0, tiled=True),
        lax.all_gather(w_down[0], "dp", axis=0, tiled=True),
    )
    gain_row = norm_gain[0]
    row_count = replay.shape[0]
    width = replay.shape[1]
    vocab_size = action_table.shape[0]
    local_ids = state_ids - lax.axis_index("dp") * row_count
    picked = jnp.take(replay, local_ids, axis=0)
    taken_hot = (sampled[:, 0:1] == jnp.arange(vocab_size)[None, :]).astype(jnp.bfloat16)
    start_state = (
        picked.astype(jnp.float32)
        + jnp.dot(taken_hot, action_table, preferred_element_type=jnp.float32)
    ).astype(jnp.bfloat16)
    pieces = 1
    piece_rows = row_count // pieces
    start_blocks = start_state.reshape(pieces, piece_rows, width)
    kept_inputs = jnp.zeros_like(start_blocks)
    final_blocks = jnp.zeros_like(start_blocks)
    arriving = jnp.zeros_like(start_blocks[0])
    for moment in range(pieces + section_count - 1):
        block_num = moment - section_pos
        usable = (block_num >= 0) & (block_num < pieces)
        block_pos = jnp.clip(block_num, 0, pieces - 1)
        source = jnp.where(
            section_pos == 0,
            lax.dynamic_index_in_dim(start_blocks, block_pos, 0, keepdims=False),
            arriving,
        )
        kept_inputs = store_block(kept_inputs, block_pos, source, usable)
        result, _ = layer_forward(source, gain_row, up_proj, down_proj)
        final_blocks = store_block(
            final_blocks, block_pos, result, usable & (section_pos == final_section)
        )
        arriving = passed_along(result, "section", 1)
    final_states = final_blocks.reshape(row_count, width)
    scale = math.sqrt(width)
    scores = contract_last(final_states, action_table) / scale
    action_hot = (sampled[:, :, None] == jnp.arange(vocab_size)[None, None, :]).astype(jnp.float32)
    chosen = jnp.einsum("ra,rka->rk", scores, action_hot, precision=lax.Precision.HIGHEST)
    loss_sum, d_chosen = head_tail(chosen, targets, scale)
    d_scores = jnp.einsum(
        "rk,rka->ra", d_chosen, action_hot, precision=lax.Precision.HIGHEST
    ).astype(jnp.bfloat16)
    grad_final = jnp.dot(d_scores, action_table, preferred_element_type=jnp.float32).astype(
        jnp.bfloat16
    )
    grad_blocks = grad_final.reshape(pieces, piece_rows, width)
    loss_part = jnp.where(section_pos == final_section, loss_sum, jnp.float32(0.0))
    ff_width = up_proj.shape[1]
    gain_sum = jnp.zeros((width,), jnp.float32)
    kept_normed = jnp.zeros((pieces, piece_rows, width), jnp.bfloat16)
    kept_upper = jnp.zeros((pieces, piece_rows, ff_width), jnp.bfloat16)
    kept_active = jnp.zeros((pieces, piece_rows, ff_width), jnp.bfloat16)
    kept_grads = jnp.zeros((pieces, piece_rows, width), jnp.bfloat16)
    arriving_grad = jnp.zeros_like(grad_blocks[0])
    for moment in range(pieces + section_count - 1):
        block_num = moment - (final_section - section_pos)
        usable = (block_num >= 0) & (block_num < pieces)
        block_pos = jnp.clip(block_num, 0, pieces - 1)
        grad_out = jnp.where(
            section_pos == final_section,
            lax.dynamic_index_in_dim(grad_blocks, block_pos, 0, keepdims=False),
            arriving_grad,
        )
        grad_out = jnp.where(usable, grad_out, jnp.zeros_like(grad_out))
        source = lax.dynamic_index_in_dim(kept_inputs, block_pos, 0, keepdims=False)
        _, cache = layer_forward(source, gain_row, up_proj, down_proj)
        grad_in, grad_upper, gain_term = layer_backward(
            grad_out, cache, gain_row, up_proj, down_proj
        )
        gain_sum = gain_sum + gain_term
        kept_normed = store_block(kept_normed, block_pos, cache[2], usable)
        kept_upper = store_block(kept_upper, block_pos, grad_upper, usable)
        kept_active = store_block(kept_active, block_pos, cache[5], usable)
        kept_grads = store_block(kept_grads, block_pos, grad_out, usable)
        arriving_grad = passed_along(grad_in, "section", -1)
    normed_flat = kept_normed.reshape(row_count, width)
    upper_flat = kept_upper.reshape(row_count, ff_width)
    active_flat = kept_active.reshape(row_count, ff_width)
    grads_flat = kept_grads.reshape(row_count, width)
    columns = normed_flat
    grad_up_part = lax.psum_scatter(
        contract_first(columns, upper_flat), "dp", scatter_dimension=0, tiled=True
    )
    columns = active_flat
    grad_down_part = lax.psum_scatter(
        contract_first(columns, grads_flat), "dp", scatter_dimension=0, tiled=True
    )
    gain_total = lax.psum(gain_sum, "dp")
    loss_total = lax.psum(loss_part, ("section", "dp"))
    return (grad_up_part[None], grad_down_part[None], gain_total[None], loss_total)


def solution(mesh):
    return jax.shard_map(
        on_device,
        mesh=mesh,
        in_specs=(
            P("dp", None),
            P("dp"),
            P("dp", None),
            P("dp"),
            P(),
            P("section", None),
            P("section", "dp", None),
            P("section", "dp", None),
        ),
        out_specs=(P("section", "dp", None), P("section", "dp", None), P("section", None), P()),
        check_vma=False,
    )
```

profile of v0, /device:TPU:0, one launch (start us, length us, event | category | flops | bytes accessed | tf_op | source)
XLA Modules:
  0.0 579.1 jit_solution(6488218659815858036)
XLA Ops:
  9.4 4.6 gather_fusion
  14.0 2.1 fusion.22
  16.2 73.0 %all-gather.5.cloned.1.call-done = bf16[1,4096,512]{2,1,0:T(8,128)(2,1)} async-done(((bf16[1,256,512]{2,1,0:T(8,128)(2,1)}), bf16[1,4096,512]{2,1,0:T(8,128)(2,1)}) %all-gather.5.cloned.1.call-update) | async-done | bytes 4194320 | tf_op jit(solution)/shard_map/all_gather | solution.py:84
  89.1 77.0 %all-gather.7.cloned.1.call-done = bf16[1,512,4096]{2,1,0:T(8,128)(2,1)} async-done(((bf16[1,32,4096]{2,1,0:T(8,128)(2,1)}), bf16[1,512,4096]{2,1,0:T(8,128)(2,1)}) %all-gather.7.cloned.1.call-update) | async-done | bytes 4194320 | tf_op jit(solution)/shard_map/all_gather | solution.py:85
  166.1 6.0 %fusion.2 = bf16[128,4096]{1,0:T(8,128)(2,1)} fusion(bf16[1,512,4096]{2,1,0:T(8,128)(2,1)} %all-gather.7.cloned.1.call-done, bf16[128,4096]{1,0:T(8,128)(2,1)S(1)} %get-tuple-element.17, pred[]{:T(512)S(6)} %eq.24, bf16[1,4096,512]{2,1,0:T(8,128)(2,1)} %all-gather.5.cloned.1.call-done, f32[4096]{0:T(1024)S(1)} %bitcast.78, f32[128]{0:T(128)S(1)} %add_rsqrt_fusion.2), kind=kOutput, calls=%fused_computation.7 | convolution fusion | flops 1078788096 | bytes 10502657 | tf_op jit(solution)/shard_map/dot_general | solution.py:40
  172.1 2.3 collective-permute-start
  174.5 1.5 collective-permute-done
  176.4 2.4 fusion.28
  180.3 4.2 fusion.66
  184.4 1.8 fusion.21
  187.1 1.5 fusion.20
  190.1 1.6 copy-done.20
  191.6 1.5 fusion.60
  193.2 2.2 fusion.36
  195.4 1.9 fusion.33
  198.6 3.6 collective-permute-done.1
  202.2 6.1 %fusion.72 = f32[512,4096]{1,0:T(8,128)} fusion(pred[]{:T(512)S(6)} %and.29, pred[]{:T(512)S(6)} %and.25, bf16[128,4096]{1,0:T(8,128)(2,1)} %copy-done.1, pred[]{:T(512)S(6)} %eq.57, bf16[128,4096]{1,0:T(8,128)(2,1)} %collective-permute-done.1, f32[128,512]{1,0:T(8,128)S(1)} %fusion.14), kind=kOutput, calls=%fused_computation.67 | convolution fusion | flops 540475392 | bytes 10747907 | tf_op jit(solution)/shard_map/dot_general | solution.py:28
  208.6 4.0 fusion.57
  213.3 4.6 fusion.69
  219.8 44.2 %psum.15 = f32[]{:T(128)} all-reduce(f32[]{:T(128)S(6)} %select_n.174), channel_id=1, replica_groups=mesh['section'=2,'dp'=16] {'section','dp'}, use_global_device_ids=true, to_apply=%region_12.13 | all-reduce | flops 1 | bytes 8 | tf_op jit(solution)/shard_map/psum | solution.py:174
  264.0 3.7 fusion.39
  267.7 78.2 %psum.14 = f32[1,4096]{1,0:T(1,128)} all-reduce(f32[1,4096]{1,0:T(1,128)S(1)} %bitcast.84), channel_id=1, replica_groups=mesh['section'=2,'dp'=16] {'dp'}, use_global_device_ids=true, to_apply=%region_9.10 | all-reduce | flops 4096 | bytes 32768 | tf_op jit(solution)/shard_map/psum | solution.py:173
  345.9 42.7 %reduce-scatter.5.cloned.1.call-done = f32[32,4096]{1,0:T(8,128)} async-done(((f32[512,4096]{1,0:T(8,128)}), f32[32,4096]{1,0:T(8,128)}) %reduce-scatter.5.cloned.1.call-update) | async-done | bytes 524304 | tf_op jit(solution)/shard_map/reduce_scatter | solution.py:170
  388.7 183.8 %reduce-scatter.3.cloned.1.call-done = f32[256,512]{1,0:T(8,128)} async-done(((f32[4096,512]{1,0:T(8,128)}), f32[256,512]{1,0:T(8,128)}) %reduce-scatter.3.cloned.1.call-update) | async-done | bytes 524304 | tf_op jit(solution)/shard_map/reduce_scatter | solution.py:166
  (68 shorter events, 9.8 us)
Async XLA Ops:
  7.2 6.9 %copy-start = (bf16[256,4096]{1,0:T(8,128)(2,1)S(1)}, bf16[256,4096]{1,0:T(8,128)(2,1)}, u32[]{:S(2)}) copy-start(bf16[256,4096]{1,0:T(8,128)(2,1)} %param.12) | copy-start | bytes 6291460
  7.2 81.9 %all-gather.5.cloned.1.call-start = ((), (), s32[]{:S(2)}) async-start(), calls=%async_computation.4 | async-start | bytes 4456448 | tf_op jit(solution)/shard_map/all_gather | solution.py:84
  7.9 158.2 %all-gather.7.cloned.1.call-start = ((), (), s32[]{:S(2)}) async-start(), calls=%async_computation.5 | async-start | bytes 4456448 | tf_op jit(solution)/shard_map/all_gather | solution.py:85
  8.7 380.0 %reduce-scatter.5.cloned.1.call-start = ((), (), s32[]{:S(2)}) async-start(), calls=%async_computation.3 | async-start | bytes 8912896 | tf_op jit(solution)/shard_map/reduce_scatter | solution.py:170
  9.4 4.6 copy-start.10
  14.0 152.1 %copy-start.6 = (f32[1,4096]{1,0:T(1,128)S(1)}, f32[1,4096]{1,0:T(1,128)}, u32[]{:S(2)}) copy-start(f32[1,4096]{1,0:T(1,128)} %param.13) | copy-start | bytes 49156
  16.1 159.8 %copy-start.4 = (bf16[128,4096]{1,0:T(8,128)(2,1)}, bf16[128,4096]{1,0:T(8,128)(2,1)S(1)}, u32[]{:S(2)}) copy-start(bf16[128,4096]{1,0:T(8,128)(2,1)S(1)} %get-tuple-element.17) | copy-start | bytes 3145732
  172.1 3.9 collective-permute-start
  176.0 3.5 copy-start.2
  176.4 3.0 copy-start.5
  179.4 9.7 %copy-start.11 = (f32[128]{0:T(128)}, f32[128]{0:T(128)S(1)}, u32[]{:S(2)}) copy-start(f32[128]{0:T(128)S(1)} %get-tuple-element.15) | copy-start | bytes 1540
  180.3 6.1 %copy-start.15 = (s32[128]{0:T(128)S(1)}, s32[128]{0:T(128)}, u32[]{:S(2)}) copy-start(s32[128]{0:T(128)} %param.11) | copy-start | bytes 1540
  187.0 2.1 copy-start.16
  187.1 2.2 copy-start.3
  189.1 6.3 %copy-start.1 = (bf16[128,4096]{1,0:T(8,128)(2,1)}, bf16[128,4096]{1,0:T(8,128)(2,1)S(1)}, u32[]{:S(2)}) copy-start(bf16[128,4096]{1,0:T(8,128)(2,1)S(1)} %convolution_convert_fusion) | copy-start | bytes 3145732
  189.3 2.3 copy-start.20
  191.6 1.5 copy-start.12
  193.2 2.2 copy-start.18
  197.3 4.9 collective-permute-start.1
  208.3 364.2 %reduce-scatter.3.cloned.1.call-start = ((), (), s32[]{:S(2)}) async-start(), calls=%async_computation.2 | async-start | bytes 8912896 | tf_op jit(solution)/shard_map/reduce_scatter | solution.py:166
  208.6 4.7 copy-start.13
  217.9 46.1 %copy-start.8 = (bf16[128,512]{1,0:T(8,128)(2,1)S(1)}, bf16[128,512]{1,0:T(8,128)(2,1)}, u32[]{:S(2)}) copy-start(bf16[128,512]{1,0:T(8,128)(2,1)} %copy-done.7) | copy-start | bytes 393220
  217.9 46.1 %copy-start.14 = (f32[128]{0:T(128)S(1)}, f32[128]{0:T(128)}, u32[]{:S(2)}) copy-start(f32[128]{0:T(128)} %copy-done.11) | copy-start | bytes 1540
  264.0 3.7 copy-start.9
  (3 other events, 1.9 us)
Sparse Core Ops, SparseCore 0:
  10.8 78.3 all-gather.4
  91.9 74.1 all-gather.6
  208.4 180.2 reduce-scatter.4
  391.4 181.0 reduce-scatter.2
where the time goes:
time: 581 us; the launch traced here: 579 us
  waiting for transfers between devices  383 us (66%)
  blocking collectives  122 us (21%)
  matrix products  39.8 us (7%)
  between operations  14.7 us (3%)
  local copies, waits for them, and re-layouts  8.01 us (1%)
  other arithmetic  7.24 us (1%)
    reduce_scatter x1, waiting for transfers between devices, on_device(): lax.psum_scatter(contract_first(columns, upper_flat), 'dp', scatter_dimen...  184 us
    psum x1, blocking collectives, on_device(): gain_total = lax.psum(gain_sum, 'dp')  78.2 us
    all_gather x1, waiting for transfers between devices, on_device(): lax.all_gather(w_down[0], 'dp', axis=0, tiled=True)  77 us
    all_gather x1, waiting for transfers between devices, on_device(): lax.all_gather(w_up[0], 'dp', axis=0, tiled=True)  73 us
    psum x1, blocking collectives, on_device(): loss_total = lax.psum(loss_part, ('section', 'dp'))  44.2 us
    reduce_scatter x1, waiting for transfers between devices, on_device(): lax.psum_scatter(contract_first(columns, grads_flat), 'dp', scatter_dimen...  42.7 us
    dot_general x5, matrix products, contract_last(): lax.dot_general(left, right, (((1,), (1,)), ((), ())), preferred_element_...  15.7 us
  transfers between devices with their start and end apart: 6, of which 6 were waited for; matrix products, arithmetic and copies ran while one was open for 4% of the time, Pallas kernels for 0%

commit v1 on v0

v1 whole, which is shorter than its diff:
```python
import functools
import math

import jax
import jax.numpy as jnp
from jax import lax
from jax.experimental import pallas as pl
from jax.experimental.pallas import tpu as pltpu
from jax.sharding import PartitionSpec as P

ROWS_DEV = 128
epsilon = 1e-06
logit_cap = 15.0
bf16 = jnp.bfloat16
f32 = jnp.float32


def contract_last(left, right):
    return lax.dot_general(left, right, (((1,), (1,)), ((), ())), preferred_element_type=f32)


def contract_first(left, right):
    return lax.dot_general(left, right, (((0,), (0,)), ((), ())), preferred_element_type=f32)


def dot(left, right):
    return jnp.dot(left, right, preferred_element_type=f32)


def exchange_kernel(size, place, kinds, *refs):
    count = len(kinds)
    ins, outs = refs[:count], refs[count : 2 * count]
    send_sem, recv_sem, own_sem = refs[2 * count :]
    me, target = place()
    barrier = pltpu.get_barrier_semaphore()
    for k in range(1, size):
        pl.semaphore_signal(
            barrier,
            inc=1,
            device_id=target(lax.rem(me + k, size)),
            device_id_type=pl.DeviceIdType.MESH,
        )
    pl.semaphore_wait(barrier, size - 1)
    copies = []
    for a in range(count):
        for k in range(1, size):
            peer = lax.rem(me + k, size)
            copies.append(
                pltpu.make_async_remote_copy(
                    src_ref=ins[a] if kinds[a] else ins[a].at[peer],
                    dst_ref=outs[a].at[me],
                    send_sem=send_sem.at[a, k],
                    recv_sem=recv_sem.at[a, k],
                    device_id=target(peer),
                    device_id_type=pl.DeviceIdType.MESH,
                )
            )
            copies[-1].start()
    own = []
    for a in range(count):
        own.append(
            pltpu.make_async_copy(
                ins[a] if kinds[a] else ins[a].at[me], outs[a].at[me], own_sem.at[a]
            )
        )
        own[-1].start()
    for copy in own:
        copy.wait()
    for copy in copies:
        copy.wait()


class Groups:
    def __init__(self, sections, devices):
        self.sections = sections
        outer = 1
        while outer * outer < devices:
            outer *= 2
        self.outer, self.inner = outer, devices // outer
        self.calls = 0

    def place_outer(self):
        pos = lax.axis_index("dp")
        low = lax.rem(pos, self.inner)
        return lax.div(pos, self.inner), lambda p: {"dp": p * self.inner + low}

    def place_inner(self):
        pos = lax.axis_index("dp")
        low = lax.rem(pos, self.inner)
        return low, lambda p: {"dp": pos - low + p}

    def place_section(self):
        return lax.axis_index("section"), lambda p: {"section": p}

    def run(self, size, place, gathers, swaps):
        arrays = list(gathers) + list(swaps)
        kinds = [True] * len(gathers) + [False] * len(swaps)
        shapes = [
            jax.ShapeDtypeStruct(((size,) + x.shape) if g else x.shape, x.dtype)
            for x, g in zip(arrays, kinds)
        ]
        ident = self.calls
        self.calls += 1
        spec = pl.BlockSpec(memory_space=pltpu.VMEM)
        return pl.pallas_call(
            functools.partial(exchange_kernel, size, place, kinds),
            out_shape=shapes,
            in_specs=[spec] * len(arrays),
            out_specs=[spec] * len(arrays),
            scratch_shapes=[
                pltpu.SemaphoreType.DMA((len(arrays), size)),
                pltpu.SemaphoreType.DMA((len(arrays), size)),
                pltpu.SemaphoreType.DMA((len(arrays),)),
            ],
            compiler_params=pltpu.CompilerParams(collective_id=ident, has_side_effects=True),
        )(*arrays)

    def over_outer(self, gathers=(), swaps=()):
        return self.run(self.outer, self.place_outer, gathers, swaps)

    def over_inner(self, gathers=(), swaps=()):
        return self.run(self.inner, self.place_inner, gathers, swaps)

    def over_section(self, gathers=(), swaps=()):
        return self.run(self.sections, self.place_section, gathers, swaps)


def head_tail(chosen, targets, scale):
    bent = jnp.tanh(chosen / logit_cap)
    logits = logit_cap * bent
    expo = jnp.exp(logits)
    summed = jnp.sum(expo, -1, keepdims=True)
    target_hot = (targets[:, None] == jnp.arange(chosen.shape[1])[None, :]).astype(f32)
    cross = jnp.log(summed[:, 0]) - jnp.sum(logits * target_hot, -1)
    loss_sum = jnp.sum(cross) / ROWS_DEV
    d_logits = (expo / summed - target_hot) / ROWS_DEV
    d_chosen = d_logits * (1.0 - bent * bent) / scale
    return (loss_sum, d_chosen)


def on_device(replay, state_ids, sampled, targets, action_table, norm_gain, w_up, w_down):
    sections = lax.axis_size("section")
    groups = Groups(sections, lax.axis_size("dp"))
    outer, inner = groups.outer, groups.inner
    section_pos = lax.axis_index("section")
    dp_pos = lax.axis_index("dp")
    outer_pos = dp_pos // inner
    held_rows, width = replay.shape
    rows = held_rows // sections
    vocab = action_table.shape[0]
    cut = width // outer
    ff = w_up.shape[2]
    ff_held = w_down.shape[1]
    group_rows = outer * rows
    scale = math.sqrt(width)

    def my_rows(x):
        return lax.dynamic_slice_in_dim(x, section_pos * rows, rows, 0)

    def my_cut(x):
        return lax.dynamic_slice_in_dim(x, outer_pos * cut, cut, 1)

    def to_cuts(x):
        return x.reshape(x.shape[0], outer, cut).transpose(1, 0, 2)

    ids = my_rows(state_ids) - dp_pos * held_rows
    picks = my_rows(sampled)
    marks = my_rows(targets)
    table_cut = my_cut(action_table)
    id_hot = (ids[:, None] == jnp.arange(held_rows)[None, :]).astype(bf16)
    taken_hot = (picks[:, 0:1] == jnp.arange(vocab)[None, :]).astype(bf16)
    start = (dot(id_hot, replay) + dot(taken_hot, action_table)).astype(bf16)
    start_wide = start.astype(f32)
    start_recip = lax.rsqrt(jnp.mean(start_wide * start_wide, -1, keepdims=True) + epsilon)

    state_cuts, down_cuts = groups.over_outer(swaps=(to_cuts(start), to_cuts(w_down[0])))
    up_all, down_all = groups.over_inner(
        gathers=(w_up[0], down_cuts.reshape(outer * ff_held, cut))
    )
    up_cut = up_all.reshape(cut, ff)
    down_cut = (
        down_all.reshape(inner, outer, ff_held, cut).transpose(1, 0, 2, 3).reshape(ff, cut)
    )
    ups, downs, gains = groups.over_section(gathers=(up_cut, down_cut, my_cut(norm_gain)))

    state = state_cuts.reshape(group_rows, cut)
    kept = []
    for layer in range(sections):
        wide = state.astype(f32)
        scaled = wide * gains[layer]
        part = dot(scaled.astype(bf16), ups[layer]).astype(bf16).reshape(outer, rows, ff)
        if layer == 0:
            (parts,) = groups.over_outer(swaps=(part,))
            recip = start_recip
        else:
            squares = jnp.sum(wide * wide, -1).reshape(outer, 1, rows)
            parts, squares = groups.over_outer(swaps=(part, squares))
            recip = lax.rsqrt(jnp.sum(squares, 0).reshape(rows, 1) / width + epsilon)
        upper = jnp.sum(parts.astype(f32), 0) * recip
        active = (upper * jax.nn.sigmoid(upper)).astype(bf16)
        (actives,) = groups.over_outer(gathers=(active,))
        actives = actives.reshape(group_rows, ff)
        kept.append((state, recip, upper, actives))
        state = (wide + dot(actives, downs[layer])).astype(bf16)

    score_part = contract_last(state, table_cut).reshape(outer, rows, vocab)
    (score_parts,) = groups.over_outer(swaps=(score_part,))
    scores = jnp.sum(score_parts, 0) / scale
    hot = picks[:, :, None] == jnp.arange(vocab)[None, None, :]
    chosen = jnp.sum(jnp.where(hot, scores[:, None, :], 0.0), -1)
    loss_sum, d_chosen = head_tail(chosen, marks, scale)
    d_scores = jnp.sum(jnp.where(hot, d_chosen[:, :, None], 0.0), 1).astype(bf16)
    (d_all,) = groups.over_outer(gathers=(d_scores,))
    grad = dot(d_all.reshape(group_rows, vocab), table_cut).astype(bf16)

    grads_up, grads_down, grads_gain = [], [], []
    for layer in reversed(range(sections)):
        state, recip, upper, actives = kept[layer]
        part = contract_last(grad, downs[layer]).astype(bf16).reshape(outer, rows, ff)
        (parts,) = groups.over_outer(swaps=(part,))
        sigm = jax.nn.sigmoid(upper)
        d_upper = (
            jnp.sum(parts.astype(f32), 0) * sigm * (1.0 + upper * (1.0 - sigm))
        ).astype(bf16)
        pull = jnp.sum(d_upper.astype(f32) * upper, -1, keepdims=True) * recip * recip / width
        d_uppers, recips, pulls = groups.over_outer(
            gathers=(d_upper, recip.reshape(1, rows), pull.reshape(1, rows))
        )
        d_uppers = d_uppers.reshape(group_rows, ff)
        recips = recips.reshape(group_rows, 1)
        pulls = pulls.reshape(group_rows, 1)
        wide = state.astype(f32)
        ready = wide * recips
        d_normed = contract_last(d_uppers, ups[layer])
        grads_gain.append(jnp.sum(d_normed * ready, 0))
        normed = (ready * gains[layer]).astype(bf16)
        grads_up.append(contract_first(normed, d_uppers).astype(bf16))
        grads_down.append(contract_first(actives, grad).astype(bf16))
        if layer:
            grad = (
                grad.astype(f32) + d_normed * gains[layer] * recips - wide * pulls
            ).astype(bf16)

    gain_rows = jnp.stack(grads_gain[::-1])[:, None, :]
    loss_rows = jnp.broadcast_to(loss_sum, (sections, 1, 128))
    small = jnp.concatenate([gain_rows, loss_rows], -1)
    up_got, down_got, small_got = groups.over_section(
        swaps=(jnp.stack(grads_up[::-1]), jnp.stack(grads_down[::-1]), small)
    )
    up_mine = jnp.sum(up_got.astype(f32), 0).astype(bf16).reshape(inner, cut // inner, ff)
    down_mine = (
        jnp.sum(down_got.astype(f32), 0)
        .astype(bf16)
        .reshape(outer, inner, ff_held, cut)
        .transpose(1, 0, 2, 3)
        .reshape(inner, outer * ff_held, cut)
    )
    small_got, up_got, down_got = groups.over_inner(
        gathers=(jnp.sum(small_got, 0),), swaps=(up_mine, down_mine)
    )
    grad_up = jnp.sum(up_got.astype(f32), 0)
    down_full = jnp.sum(down_got.astype(f32), 0).astype(bf16).reshape(outer, ff_held, cut)
    small_got, down_got = groups.over_outer(
        gathers=(jnp.sum(small_got, 0),), swaps=(down_full,)
    )
    grad_down = down_got.transpose(1, 0, 2).reshape(ff_held, width).astype(f32)
    grad_gain = small_got[:, 0, :cut].reshape(1, width)
    loss = jnp.sum(small_got[:, 0, cut])
    return (grad_up[None], grad_down[None], grad_gain, loss)


def solution(mesh):
    return jax.shard_map(
        on_device,
        mesh=mesh,
        in_specs=(
            P("dp", None),
            P("dp"),
            P("dp", None),
            P("dp"),
            P(),
            P("section", None),
            P("section", "dp", None),
            P("section", "dp", None),
        ),
        out_specs=(P("section", "dp", None), P("section", "dp", None), P("section", None), P()),
        check_vma=False,
    )
```

time: 581 us -> 277 us (0.48)
  waiting for transfers between devices: 383 us -> 0 us
  Pallas kernels: 0 us -> 205 us
  blocking collectives: 122 us -> 0 us
  other arithmetic: 7.24 us -> 33.5 us
  matrix products: 39.8 us -> 21.3 us
  between operations: 14.7 us -> 1.75 us
  local copies, waits for them, and re-layouts: 8.01 us -> 14.3 us
    reduce_scatter x2 -> x0, waiting for transfers between devices: 227 us -> none  [the longest x1 184 us: on_device(): lax.psum_scatter(contract_first(columns, upper_flat), 'dp', scatter_dimen...]
    pallas_call x0 -> x16, Pallas kernels: none -> 205 us  [run(): pl.pallas_call(functools.partial(exchange_kernel, size, place, kinds), ou...]
    all_gather x2 -> x0, waiting for transfers between devices: 150 us -> none  [the longest x1 77 us: on_device(): lax.all_gather(w_down[0], 'dp', axis=0, tiled=True)]
    psum x2 -> x0, blocking collectives: 122 us -> none  [the longest x1 78.2 us: on_device(): gain_total = lax.psum(gain_sum, 'dp')]
    reduce_sum x2 -> x17, other arithmetic: 2.9 us -> 20.1 us  [the longest x1 3.31 us: on_device(): jnp.sum(up_got.astype(f32), 0).astype(bf16).reshape(inner, cut // inner, ff)]
    dot_general x2 -> x4, matrix products: 10.7 us -> 2.02 us  [contract_first(): lax.dot_general(left, right, (((0,), (0,)), ((), ())), preferred_element_...]
    dot_general x7 -> x6, matrix products: 13.4 us -> 8.92 us  [dot(): return jnp.dot(left, right, preferred_element_type=f32)]
  transfers between devices with their start and end apart: 6 -> 0, of which waited for: 6 -> 0; matrix products, arithmetic and copies ran while one was open for 4% -> 0% of each run, Pallas kernels for 0% -> 0%
where the time goes in v1:
time: 277 us; the launch traced here: 276 us
  Pallas kernels  205 us (74%)
  other arithmetic  33.5 us (12%)
  matrix products  21.3 us (8%)
  local copies, waits for them, and re-layouts  14.3 us (5%)
    pallas_call x16, Pallas kernels, run(): pl.pallas_call(functools.partial(exchange_kernel, size, place, kinds), ou...  205 us
    dot_general x5, matrix products, contract_last(): lax.dot_general(left, right, (((1,), (1,)), ((), ())), preferred_element_...  10.4 us
    dot_general x6, matrix products, dot(): return jnp.dot(left, right, preferred_element_type=f32)  8.92 us

profile of v1, /device:TPU:0, one launch (start us, length us, event | category | flops | bytes accessed | tf_op | source)
XLA Modules:
  0.0 275.6 jit_solution(9390553147566735558)
XLA Ops:
  6.9 23.7 %shard_map.111 = (bf16[4,64,1024]{2,1,0:T(8,128)(2,1)}, bf16[4,32,1024]{2,1,0:T(8,128)(2,1)}) custom-call(bf16[4,64,1024]{2,1,0:T(8,128)(2,1)} %bitcast.115, bf16[4,32,1024]{2,1,0:T(8,128)(2,1)} %bitcast.123), custom_call_target="tpu_custom_call" | custom-call | tf_op jit(solution)/shard_map/pallas_call | solution.py:105
  30.7 28.6 %shard_map.112 = (bf16[4,256,512]{2,1,0:T(8,128)(2,1)}, bf16[4,128,1024]{2,1,0:T(8,128)(2,1)}) custom-call(bf16[256,512]{1,0:T(8,128)(2,1)} %bitcast.131, bf16[128,1024]{1,0:T(8,128)(2,1)} %bitcast.132), custom_call_target="tpu_custom_call" | custom-call | tf_op jit(solution)/shard_map/pallas_call | solution.py:105
  59.2 2.4 copy.22
  61.6 7.8 %shard_map.113 = (bf16[2,1024,512]{2,1,0:T(8,128)(2,1)}, bf16[2,512,1024]{2,1,0:T(8,128)(2,1)}, f32[2,1,1024]{2,1,0:T(1,128)}) custom-call(bf16[1024,512]{1,0:T(8,128)(2,1)} %bitcast.124, bf16[512,1024]{1,0:T(8,128)(2,1)} %bitcast.113, f32[1,1024]{1,0:T(1,128)} %constant_dynamic-slice_fusion.1.refs_2_), custom_call_target="tpu_custom_call" | custom-call | tf_op jit(solution)/shard_map/pallas_call | solution.py:105
  70.3 2.4 convolution_convert_fusion.7
  72.6 10.8 %shard_map.114 = bf16[4,64,512]{2,1,0:T(8,128)(2,1)} custom-call(bf16[4,64,512]{2,1,0:T(8,128)(2,1)} %bitcast.134), custom_call_target="tpu_custom_call" | custom-call | tf_op jit(solution)/shard_map/pallas_call | solution.py:105
  85.7 8.8 %shard_map.115 = bf16[4,64,512]{2,1,0:T(8,128)(2,1)} custom-call(bf16[64,512]{1,0:T(8,128)(2,1)} %multiply_convert_fusion.6.refs_0_), custom_call_target="tpu_custom_call" | custom-call | tf_op jit(solution)/shard_map/pallas_call | solution.py:105
  98.4 10.0 %shard_map.116 = (bf16[4,64,512]{2,1,0:T(8,128)(2,1)}, f32[4,1,64]{2,1,0:T(1,128)}) custom-call(bf16[4,64,512]{2,1,0:T(8,128)(2,1)} %bitcast.133, f32[4,1,64]{2,1,0:T(1,128)} %reshape.276.refs_1_), custom_call_target="tpu_custom_call" | custom-call | tf_op jit(solution)/shard_map/pallas_call | solution.py:105
  111.3 8.5 %shard_map.117 = bf16[4,64,512]{2,1,0:T(8,128)(2,1)} custom-call(bf16[64,512]{1,0:T(8,128)(2,1)} %multiply_convert_fusion.5.refs_0_), custom_call_target="tpu_custom_call" | custom-call | tf_op jit(solution)/shard_map/pallas_call | solution.py:105
  119.8 2.7 fusion.10
  122.5 9.2 %shard_map.118 = f32[4,64,256]{2,1,0:T(8,128)} custom-call(f32[4,64,256]{2,1,0:T(8,128)} %bitcast.136), custom_call_target="tpu_custom_call" | custom-call | tf_op jit(solution)/shard_map/pallas_call | solution.py:105
  135.7 7.9 %shard_map.119 = bf16[4,64,256]{2,1,0:T(8,128)(2,1)} custom-call(bf16[64,256]{1,0:T(8,128)(2,1)} %select_reduce_fusion.refs_0_), custom_call_target="tpu_custom_call" | custom-call | tf_op jit(solution)/shard_map/pallas_call | solution.py:105
  144.8 2.4 convolution_convert_fusion.5
  147.3 10.8 %shard_map.120 = bf16[4,64,512]{2,1,0:T(8,128)(2,1)} custom-call(bf16[4,64,512]{2,1,0:T(8,128)(2,1)} %bitcast.137), custom_call_target="tpu_custom_call" | custom-call | tf_op jit(solution)/shard_map/pallas_call | solution.py:105
  160.5 9.9 %shard_map.121 = (bf16[4,64,512]{2,1,0:T(8,128)(2,1)}, f32[4,1,64]{2,1,0:T(1,128)}, f32[4,1,64]{2,1,0:T(1,128)}) custom-call(bf16[64,512]{1,0:T(8,128)(2,1)} %get-tuple-element.53.refs_0_, f32[1,64]{1,0:T(1,128)} %get-tuple-element.60.refs_1_, f32[1,64]{1,0:T(1,128)} %fusion.50.refs_2_), custom_call_target="tpu_custom_call" | custom-call | tf_op jit(solution)/shard_map/pallas_call | solution.py:105
  173.8 2.2 fusion.12
  178.0 9.9 %shard_map.122 = bf16[4,64,512]{2,1,0:T(8,128)(2,1)} custom-call(bf16[4,64,512]{2,1,0:T(8,128)(2,1)} %bitcast.135), custom_call_target="tpu_custom_call" | custom-call | tf_op jit(solution)/shard_map/pallas_call | solution.py:105
  190.3 10.1 %shard_map.123 = (bf16[4,64,512]{2,1,0:T(8,128)(2,1)}, f32[4,1,64]{2,1,0:T(1,128)}, f32[4,1,64]{2,1,0:T(1,128)}) custom-call(bf16[64,512]{1,0:T(8,128)(2,1)} %get-tuple-element.51.refs_0_, f32[1,64]{1,0:T(1,128)} %get-tuple-element.58.refs_1_, f32[1,64]{1,0:T(1,128)} %fusion.51.refs_2_), custom_call_target="tpu_custom_call" | custom-call | tf_op jit(solution)/shard_map/pallas_call | solution.py:105
  210.2 8.4 %shard_map.124 = (bf16[2,1024,512]{2,1,0:T(8,128)(2,1)}, bf16[2,512,1024]{2,1,0:T(8,128)(2,1)}, f32[2,1,1152]{2,1,0:T(1,128)}) custom-call(bf16[2,1024,512]{2,1,0:T(8,128)(2,1)} %pad_maximum_fusion.refs_0_, bf16[2,512,1024]{2,1,0:T(8,128)(2,1)} %pad_maximum_fusion.1.refs_1_, f32[2,1,1152]{2,1,0:T(1,128)} %concatenate.3.refs_2_), custom_call_target="tpu_custom_call" | custom-call | tf_op jit(solution)/shard_map/pallas_call | solution.py:105
  221.9 3.3 %reduce_sum.254 = bf16[1024,512]{1,0:T(8,128)(2,1)} reduce(bf16[2,1024,512]{2,1,0:T(8,128)(2,1)} %get-tuple-element.41, bf16[]{:T(256)} %constant.65.clone.1), dimensions={0}, to_apply=%region_18.19 | reduce | flops 524288 | bytes 3145730 | tf_op jit(solution)/shard_map/reduce_sum | solution.py:250
  225.8 29.4 %shard_map.125 = (f32[4,1,1152]{2,1,0:T(1,128)}, bf16[4,256,512]{2,1,0:T(8,128)(2,1)}, bf16[4,128,1024]{2,1,0:T(8,128)(2,1)}) custom-call(f32[1,1152]{1,0:T(1,128)} %reduce_sum.253.refs_0_, bf16[4,256,512]{2,1,0:T(8,128)(2,1)} %bitcast.112, bf16[4,128,1024]{2,1,0:T(8,128)(2,1)} %bitcast.111), custom_call_target="tpu_custom_call" | custom-call | tf_op jit(solution)/shard_map/pallas_call | solution.py:105
  255.3 2.2 reduce_sum.259
  258.8 10.9 %shard_map.126 = (f32[4,1,1152]{2,1,0:T(1,128)}, bf16[4,32,1024]{2,1,0:T(8,128)(2,1)}) custom-call(f32[1,1152]{1,0:T(1,128)} %reduce_sum.258.refs_0_, bf16[4,32,1024]{2,1,0:T(8,128)(2,1)} %bitcast.122), custom_call_target="tpu_custom_call" | custom-call | tf_op jit(solution)/shard_map/pallas_call | solution.py:105
  273.4 2.2 convert_reduce_fusion
  (102 shorter events, 49.3 us)
Async XLA Ops:
  0.6 3.9 %copy-start = (bf16[256,4096]{1,0:T(8,128)(2,1)S(1)}, bf16[256,4096]{1,0:T(8,128)(2,1)}, u32[]{:S(2)}) copy-start(bf16[256,4096]{1,0:T(8,128)(2,1)} %param.12) | copy-start | bytes 6291460
  0.6 3.8 %copy-start.11 = (s32[128,20]{0,1:T(8,128)S(1)}, s32[128,20]{0,1:T(8,128)}, u32[]{:S(2)}) copy-start(s32[128,20]{0,1:T(8,128)} %param.10) | copy-start | bytes 30724
  4.5 1.5 copy-start.9
  59.2 10.9 %copy-start.1 = (bf16[4,64,1024]{2,1,0:T(8,128)(2,1)S(1)}, bf16[4,64,1024]{2,1,0:T(8,128)(2,1)}, u32[]{:S(2)}) copy-start(bf16[4,64,1024]{2,1,0:T(8,128)(2,1)} %get-tuple-element.26) | copy-start | bytes 1572868
  94.5 2.0 copy-start.14
  96.5 26.0 %copy-start.4 = (bf16[256,1024]{1,0:T(8,128)(2,1)}, bf16[256,1024]{1,0:T(8,128)(2,1)S(1)}, u32[]{:S(2)}) copy-start(bf16[256,1024]{1,0:T(8,128)(2,1)S(1)} %get-tuple-element.65) | copy-start | bytes 1572868
  119.8 13.5 %copy-start.17 = (s32[128]{0:T(128)S(1)}, s32[128]{0:T(128)}, u32[]{:S(2)}) copy-start(s32[128]{0:T(128)} %param.11) | copy-start | bytes 1540
  173.8 3.0 %copy-start.15 = (bf16[2,512,1024]{2,1,0:T(8,128)(2,1)S(1)}, bf16[2,512,1024]{2,1,0:T(8,128)(2,1)}, u32[]{:S(2)}) copy-start(bf16[2,512,1024]{2,1,0:T(8,128)(2,1)} %get-tuple-element.32) | copy-start | bytes 6291460
  176.0 0.8 copy-start.6
  189.7 14.8 %copy-start.2 = (bf16[4,64,512]{2,1,0:T(8,128)(2,1)S(1)}, bf16[4,64,512]{2,1,0:T(8,128)(2,1)}, u32[]{:S(2)}) copy-start(bf16[4,64,512]{2,1,0:T(8,128)(2,1)} %shard_map.115) | copy-start | bytes 786436
  201.9 2.6 copy-start.7
  202.0 3.0 %copy-start.3 = (bf16[4,64,512]{2,1,0:T(8,128)(2,1)S(1)}, bf16[4,64,512]{2,1,0:T(8,128)(2,1)}, u32[]{:S(2)}) copy-start(bf16[4,64,512]{2,1,0:T(8,128)(2,1)} %shard_map.117) | copy-start | bytes 786436
  205.5 1.6 copy-start.13
  205.5 1.6 copy-start.16
  207.0 1.0 copy-start.5
  207.0 1.1 copy-start.8
  221.9 3.3 %copy-start.12 = (f32[2,1,1152]{2,1,0:T(1,128)S(1)}, f32[2,1,1152]{2,1,0:T(1,128)}, u32[]{:S(2)}) copy-start(f32[2,1,1152]{2,1,0:T(1,128)} %get-tuple-element.40) | copy-start | bytes 27652
  269.7 2.5 copy-start.10

commit v2 on v1

v2 whole, which is shorter than its diff:
```python
import functools
import math

import jax
import jax.numpy as jnp
from jax import lax
from jax.experimental import pallas as pl
from jax.experimental.pallas import tpu as pltpu
from jax.sharding import PartitionSpec as P

ROWS_DEV = 128
epsilon = 1e-06
logit_cap = 15.0
bf16 = jnp.bfloat16
f32 = jnp.float32


def contract_last(left, right):
    return lax.dot_general(left, right, (((1,), (1,)), ((), ())), preferred_element_type=f32)


def contract_first(left, right):
    return lax.dot_general(left, right, (((0,), (0,)), ((), ())), preferred_element_type=f32)


def dot(left, right):
    return jnp.dot(left, right, preferred_element_type=f32)


def spread(rows, column, axis):
    here = lax.broadcasted_iota(jnp.int32, (rows, rows), 0)
    there = lax.broadcasted_iota(jnp.int32, (rows, rows), 1)
    wide = jnp.broadcast_to(column, (rows, rows))
    return jnp.sum(jnp.where(here == there, wide, 0.0), axis, keepdims=True)


class Group:
    def __init__(self, size, me, target):
        self.size, self.me, self.target = size, me, target

    def copy(self, k, source, dest, send_sem, recv_sem):
        peer = lax.rem(self.me + k, self.size)
        made = pltpu.make_async_remote_copy(
            src_ref=source(peer),
            dst_ref=dest,
            send_sem=send_sem,
            recv_sem=recv_sem,
            device_id=self.target(peer),
            device_id_type=pl.DeviceIdType.MESH,
        )
        made.start()
        return made

    def fan(self, source, dest, sems):
        return [
            self.copy(k, source, dest, sems.at[0, k], sems.at[1, k])
            for k in range(1, self.size)
        ]


def groups_of(outer, inner, sections):
    pos = lax.axis_index("dp")
    high, low = lax.div(pos, inner), lax.rem(pos, inner)
    return (
        Group(outer, high, lambda p: {"dp": p * inner + low}),
        Group(inner, low, lambda p: {"dp": pos - low + p}),
        Group(sections, lax.axis_index("section"), lambda p: {"section": p}),
    )


def greet(*groups):
    barrier = pltpu.get_barrier_semaphore()
    for group in groups:
        for k in range(1, group.size):
            pl.semaphore_signal(
                barrier,
                inc=1,
                device_id=group.target(lax.rem(group.me + k, group.size)),
                device_id_type=pl.DeviceIdType.MESH,
            )
    pl.semaphore_wait(barrier, sum(group.size - 1 for group in groups))


def local(source, dest, sem):
    made = pltpu.make_async_copy(source, dest, sem)
    made.start()
    return made


def land(copies):
    for copy in copies:
        copy.wait_recv()


def drain(copies):
    for copy in copies:
        copy.wait_send()


def stage_kernel(dims, start, down, up, gain, state, ups, downs, gains, sems, pass_sems, own_sems):
    across, within, between = groups_of(*dims)
    z, j, s = across.me, within.me, between.me
    greet(across, within, between)
    down_cuts = across.fan(lambda p: down.at[p], downs.at[s, z, j], sems.at[0])
    up_rows = within.fan(lambda p: up, ups.at[s, j], sems.at[1])
    states = across.fan(lambda p: start.at[p], state.at[z], sems.at[2])
    sent = between.fan(lambda p: gain, gains.at[s], sems.at[3])
    sent += between.fan(lambda p: up, ups.at[s, j], pass_sems.at[0, 0])
    down_own = local(down.at[z], downs.at[s, z, j], own_sems.at[0])
    own = [
        local(up, ups.at[s, j], own_sems.at[1]),
        local(start.at[z], state.at[z], own_sems.at[2]),
        local(gain, gains.at[s], own_sems.at[3]),
    ]
    down_own.wait()
    land(down_cuts)
    mine = downs.at[s, :, j]
    down_rows = within.fan(lambda p: mine, mine, sems.at[4])
    sent += between.fan(lambda p: mine, mine, pass_sems.at[1, 0])
    for number, rows in ((0, up_rows), (1, down_rows)):
        for k in range(1, within.size):
            rows[k - 1].wait_recv()
            giver = lax.rem(j + within.size - k, within.size)
            piece = ups.at[s, giver] if number == 0 else downs.at[s, :, giver]
            sent += between.fan(lambda p: piece, piece, pass_sems.at[number, k])
    land(states + sent)
    drain(down_cuts + up_rows + states + down_rows + sent)
    for copy in own:
        copy.wait()


def forward_kernel(dims, width, first, parts, stat, upper, actives, recips, recip, got, stats, row, mine, sems, own_sems):
    across, _, _ = groups_of(*dims)
    z, size = across.me, across.size
    rows = upper.shape[0]
    greet(across)
    sent = across.fan(lambda p: parts.at[p], got.at[z], sems.at[0])
    if not first:
        sent += across.fan(lambda p: stat.at[p], stats.at[z], sems.at[1])
    own = local(parts.at[z], got.at[z], own_sems.at[0])
    own.wait()
    if not first:
        own_stat = local(stat.at[z], stats.at[z], own_sems.at[1])
        own_stat.wait()
    land(sent)
    if first:
        squares = stat[...]
    else:
        squares = spread(rows, jnp.sum(stats[...], 0), 1)
    factor = lax.rsqrt(squares / width + epsilon)
    recip[...] = factor
    total = jnp.sum(got[...].astype(f32), 0) * factor
    active = (total * jax.nn.sigmoid(total)).astype(bf16)
    mine[...] = active
    row[...] = spread(rows, factor, 0)
    upper[...] = total
    more = across.fan(lambda p: mine, actives.at[z], sems.at[2])
    more += across.fan(lambda p: row, recips.at[z], sems.at[3])
    ends = [
        local(mine, actives.at[z], own_sems.at[2]),
        local(row, recips.at[z], own_sems.at[3]),
    ]
    land(more)
    drain(sent + more)
    for copy in ends:
        copy.wait()


def backward_kernel(dims, width, parts, upper, recip, d_uppers, pulls, got, row, mine, sems, own_sems):
    across, _, _ = groups_of(*dims)
    z = across.me
    rows = upper.shape[0]
    greet(across)
    sent = across.fan(lambda p: parts.at[p], got.at[z], sems.at[0])
    own = local(parts.at[z], got.at[z], own_sems.at[0])
    value = upper[...]
    sigm = jax.nn.sigmoid(value)
    slope = sigm * (1.0 + value * (1.0 - sigm))
    own.wait()
    land(sent)
    d_upper = (jnp.sum(got[...].astype(f32), 0) * slope).astype(bf16)
    mine[...] = d_upper
    factor = recip[...]
    pull = jnp.sum(d_upper.astype(f32) * value, -1, keepdims=True) * factor * factor / width
    row[...] = spread(rows, pull, 0)
    more = across.fan(lambda p: mine, d_uppers.at[z], sems.at[1])
    more += across.fan(lambda p: row, pulls.at[z], sems.at[2])
    ends = [
        local(mine, d_uppers.at[z], own_sems.at[1]),
        local(row, pulls.at[z], own_sems.at[2]),
    ]
    land(more)
    drain(sent + more)
    for copy in ends:
        copy.wait()


def head_kernel(dims, scale, parts, picks, marks, grads, loss, got, mine, sems, own_sems):
    across, _, _ = groups_of(*dims)
    z = across.me
    rows, samples = picks.shape
    vocab = parts.shape[2]
    greet(across)
    sent = across.fan(lambda p: parts.at[p], got.at[z], sems.at[0])
    own = local(parts.at[z], got.at[z], own_sems.at[0])
    own.wait()
    land(sent)
    scores = jnp.sum(got[...], 0) / scale
    actions = lax.broadcasted_iota(jnp.int32, (rows, vocab), 1)
    choice = picks[...]
    chosen = jnp.concatenate(
        [
            jnp.sum(jnp.where(choice[:, k : k + 1] == actions, scores, 0.0), -1, keepdims=True)
            for k in range(samples)
        ],
        1,
    )
    bent = jnp.tanh(chosen / logit_cap)
    logits = logit_cap * bent
    expo = jnp.exp(logits)
    summed = jnp.sum(expo, -1, keepdims=True)
    order = lax.broadcasted_iota(jnp.int32, (rows, samples), 1)
    hot = jnp.where(marks[...] == order, 1.0, 0.0)
    cross = jnp.log(summed) - jnp.sum(logits * hot, -1, keepdims=True)
    loss[...] = jnp.broadcast_to(jnp.sum(cross, 0, keepdims=True) / ROWS_DEV, loss.shape)
    d_chosen = (expo / summed - hot) / ROWS_DEV * (1.0 - bent * bent) / scale
    d_scores = jnp.zeros((rows, vocab), f32)
    for k in range(samples):
        d_scores += jnp.where(choice[:, k : k + 1] == actions, d_chosen[:, k : k + 1], 0.0)
    mine[...] = d_scores.astype(bf16)
    more = across.fan(lambda p: mine, grads.at[z], sems.at[1])
    end = local(mine, grads.at[z], own_sems.at[1])
    land(more)
    drain(sent + more)
    end.wait()


def finish_kernel(
    dims, up, down, small, grad_up, down_out, small_out,
    up_got, down_got, small_got, up_sum, down_sum, small_sum,
    up_rows, down_rows, small_rows, down_full, small_full, sems, own_sems,
):
    across, within, between = groups_of(*dims)
    z, j, s = across.me, within.me, between.me
    greet(across, within, between)

    def total(mine, got, group):
        value = mine.astype(f32)
        for k in range(1, group.size):
            value += got[k - 1].astype(f32)
        return value

    def swap(group, source, got, sems):
        return [
            group.copy(k, source, got.at[k - 1], sems.at[0, k], sems.at[1, k])
            for k in range(1, group.size)
        ]

    downs = swap(between, lambda p: down.at[p], down_got, sems.at[0])
    ups = swap(between, lambda p: up.at[p], up_got, sems.at[1])
    smalls = swap(between, lambda p: small.at[p], small_got, sems.at[2])
    land(downs)
    for part in range(across.size):
        value = down[s, part].astype(f32)
        for k in range(1, between.size):
            value += down_got[k - 1, part].astype(f32)
        down_sum[part] = value.astype(bf16)
    down_in = swap(within, lambda p: down_sum.at[:, p], down_rows, sems.at[3])
    land(smalls)
    small_sum[...] = total(small[s], small_got, between)
    small_in = swap(within, lambda p: small_sum, small_rows, sems.at[4])
    land(ups)
    for part in range(within.size):
        value = up[s, part].astype(f32)
        for k in range(1, between.size):
            value += up_got[k - 1, part].astype(f32)
        up_sum[part] = value.astype(bf16)
    up_in = swap(within, lambda p: up_sum.at[p], up_rows, sems.at[5])
    land(down_in)
    down_full[...] = total(down_sum[:, j], down_rows, within).astype(bf16)
    down_ends = across.fan(lambda p: down_full.at[p], down_out.at[z], sems.at[6])
    land(small_in)
    small_full[...] = total(small_sum[...], small_rows, within)
    small_ends = across.fan(lambda p: small_full, small_out.at[z], sems.at[7])
    own = [
        local(down_full.at[z], down_out.at[z], own_sems.at[0]),
        local(small_full, small_out.at[z], own_sems.at[1]),
    ]
    land(up_in)
    grad_up[...] = total(up_sum[j], up_rows, within)
    land(down_ends + small_ends)
    drain(downs + ups + smalls + down_in + small_in + up_in + down_ends + small_ends)
    for copy in own:
        copy.wait()


def call(ident, kernel, args, outs, scratch, sem_shapes):
    spec = pl.BlockSpec(memory_space=pltpu.VMEM)
    return pl.pallas_call(
        kernel,
        out_shape=[jax.ShapeDtypeStruct(shape, kind) for shape, kind in outs],
        in_specs=[spec] * len(args),
        out_specs=[spec] * len(outs),
        scratch_shapes=[pltpu.VMEM(shape, kind) for shape, kind in scratch]
        + [pltpu.SemaphoreType.DMA(shape) for shape in sem_shapes],
        compiler_params=pltpu.CompilerParams(collective_id=ident, has_side_effects=True),
    )(*args)


def on_device(replay, state_ids, sampled, targets, action_table, norm_gain, w_up, w_down):
    sections = lax.axis_size("section")
    devices = lax.axis_size("dp")
    outer = 1
    while outer * outer < devices:
        outer *= 2
    inner = devices // outer
    dims = (outer, inner, sections)
    top = max(dims)
    section_pos = lax.axis_index("section")
    dp_pos = lax.axis_index("dp")
    outer_pos = dp_pos // inner
    held_rows, width = replay.shape
    rows = held_rows // sections
    vocab = action_table.shape[0]
    cut = width // outer
    ff = w_up.shape[2]
    up_held = w_up.shape[1]
    ff_held = w_down.shape[1]
    group_rows = outer * rows
    scale = math.sqrt(width)
    small_width = cut + 128

    def my_rows(x):
        return lax.dynamic_slice_in_dim(x, section_pos * rows, rows, 0)

    def my_cut(x):
        return lax.dynamic_slice_in_dim(x, outer_pos * cut, cut, 1)

    def to_cuts(x):
        return x.reshape(x.shape[0], outer, cut).transpose(1, 0, 2)

    ids = my_rows(state_ids) - dp_pos * held_rows
    picks = my_rows(sampled)
    marks = my_rows(targets)
    table_cut = my_cut(action_table)
    id_hot = (ids[:, None] == jnp.arange(held_rows)[None, :]).astype(bf16)
    taken_hot = (picks[:, 0:1] == jnp.arange(vocab)[None, :]).astype(bf16)
    start = (dot(id_hot, replay) + dot(taken_hot, action_table)).astype(bf16)
    start_wide = start.astype(f32)
    squares = jnp.sum(start_wide * start_wide, -1, keepdims=True)

    state_cuts, ups, downs, gains = call(
        0,
        functools.partial(stage_kernel, dims),
        (to_cuts(start), to_cuts(w_down[0]), w_up[0], my_cut(norm_gain)),
        (
            ((outer, rows, cut), bf16),
            ((sections, inner, up_held, ff), bf16),
            ((sections, outer, inner, ff_held, cut), bf16),
            ((sections, 1, cut), f32),
        ),
        (),
        ((5, 2, top), (2, inner, 2, top), (4,)),
    )
    ups = ups.reshape(sections, cut, ff)
    downs = downs.reshape(sections, ff, cut)

    state = state_cuts.reshape(group_rows, cut)
    kept = []
    for layer in range(sections):
        wide = state.astype(f32)
        part = dot((wide * gains[layer]).astype(bf16), ups[layer]).astype(bf16)
        first = layer == 0
        stat = squares if first else jnp.sum(wide * wide, -1).reshape(outer, 1, rows)
        upper, actives, recips, recip = call(
            1 + layer,
            functools.partial(forward_kernel, dims, width, first),
            (part.reshape(outer, rows, ff), stat),
            (
                ((rows, ff), f32),
                ((outer, rows, ff), bf16),
                ((outer, 1, rows), f32),
                ((rows, 1), f32),
            ),
            (
                ((outer, rows, ff), bf16),
                ((outer, 1, rows), f32),
                ((1, rows), f32),
                ((rows, ff), bf16),
            ),
            ((4, 2, top), (4,)),
        )
        actives = actives.reshape(group_rows, ff)
        kept.append((state, recip, upper, actives, recips.reshape(group_rows, 1)))
        state = (wide + dot(actives, downs[layer])).astype(bf16)

    score_part = contract_last(state, table_cut).reshape(outer, rows, vocab)
    d_all, loss_row = call(
        1 + sections,
        functools.partial(head_kernel, dims, scale),
        (score_part, picks, marks[:, None]),
        (((outer, rows, vocab), bf16), ((1, 128), f32)),
        (((outer, rows, vocab), f32), ((rows, vocab), bf16)),
        ((2, 2, top), (2,)),
    )
    grad = dot(d_all.reshape(group_rows, vocab), table_cut).astype(bf16)

    grads_up, grads_down, grads_gain = [], [], []
    for layer in reversed(range(sections)):
        state, recip, upper, actives, recips = kept[layer]
        part = contract_last(grad, downs[layer]).astype(bf16).reshape(outer, rows, ff)
        d_uppers, pulls = call(
            2 + sections + layer,
            functools.partial(backward_kernel, dims, width),
            (part, upper, recip),
            (((outer, rows, ff), bf16), ((outer, 1, rows), f32)),
            (((outer, rows, ff), bf16), ((1, rows), f32), ((rows, ff), bf16)),
            ((3, 2, top), (3,)),
        )
        d_uppers = d_uppers.reshape(group_rows, ff)
        pulls = pulls.reshape(group_rows, 1)
        wide = state.astype(f32)
        ready = wide * recips
        d_normed = contract_last(d_uppers, ups[layer])
        grads_gain.append(jnp.sum(d_normed * ready, 0))
        normed = (ready * gains[layer]).astype(bf16)
        grads_up.append(contract_first(normed, d_uppers).astype(bf16))
        grads_down.append(contract_first(actives, grad).astype(bf16))
        if layer:
            grad = (
                grad.astype(f32) + d_normed * gains[layer] * recips - wide * pulls
            ).astype(bf16)

    gain_rows = jnp.stack(grads_gain[::-1])[:, None, :]
    loss_rows = jnp.broadcast_to(loss_row, (sections, 1, 128))
    small = jnp.concatenate([gain_rows, loss_rows], -1)
    others = sections - 1
    grad_up, down_got, small_got = call(
        2 + 2 * sections,
        functools.partial(finish_kernel, dims),
        (
            jnp.stack(grads_up[::-1]).reshape(sections, inner, up_held, ff),
            jnp.stack(grads_down[::-1]).reshape(sections, outer, inner, ff_held, cut),
            small,
        ),
        (
            ((up_held, ff), f32),
            ((outer, ff_held, cut), bf16),
            ((outer, 1, small_width), f32),
        ),
        (
            ((others, inner, up_held, ff), bf16),
            ((others, outer, inner, ff_held, cut), bf16),
            ((others, 1, small_width), f32),
            ((inner, up_held, ff), bf16),
            ((outer, inner, ff_held, cut), bf16),
            ((1, small_width), f32),
            ((inner - 1, up_held, ff), bf16),
            ((inner - 1, outer, ff_held, cut), bf16),
            ((inner - 1, 1, small_width), f32),
            ((outer, ff_held, cut), bf16),
            ((1, small_width), f32),
        ),
        ((8, 2, top), (2,)),
    )
    grad_down = down_got.transpose(1, 0, 2).reshape(ff_held, width).astype(f32)
    grad_gain = small_got[:, 0, :cut].reshape(1, width)
    loss = jnp.sum(small_got[:, 0, cut])
    return (grad_up[None], grad_down[None], grad_gain, loss)


def solution(mesh):
    return jax.shard_map(
        on_device,
        mesh=mesh,
        in_specs=(
            P("dp", None),
            P("dp"),
            P("dp", None),
            P("dp"),
            P(),
            P("section", None),
            P("section", "dp", None),
            P("section", "dp", None),
        ),
        out_specs=(P("section", "dp", None), P("section", "dp", None), P("section", None), P()),
        check_vma=False,
    )
```

time: 277 us -> 200 us (0.72)
  Pallas kernels: 205 us -> 149 us
  other arithmetic: 33.5 us -> 10.1 us
    pallas_call x16 -> x7, Pallas kernels: 205 us -> 149 us  [call(): pl.pallas_call(kernel, out_shape=[jax.ShapeDtypeStruct(shape, kind) for s...]
    reduce_sum x18 -> x0, other arithmetic: 20.2 us -> none  [the longest x1 3.31 us: on_device(): jnp.sum(up_got.astype(f32), 0).astype(bf16).reshape(inner, cut // inner, ff)]
    slice x1 -> x4, local copies, waits for them, and re-layouts: 0.69 us -> 5.68 us  [the longest x1 2.81 us: on_device(): state = (wide + dot(actives, downs[layer])).astype(bf16)]
    dot_general x4, matrix products: 2.02 us -> 5.33 us  [contract_first(): lax.dot_general(left, right, (((0,), (0,)), ((), ())), preferred_element_...]
where the time goes in v2:
time: 200 us; the launch traced here: 198 us
  Pallas kernels  149 us (74%)
  matrix products  20.8 us (10%)
  local copies, waits for them, and re-layouts  16.9 us (8%)
  other arithmetic  10.1 us (5%)
    pallas_call x7, Pallas kernels, call(): pl.pallas_call(kernel, out_shape=[jax.ShapeDtypeStruct(shape, kind) for s...  149 us
    dot_general x5, matrix products, contract_last(): lax.dot_general(left, right, (((1,), (1,)), ((), ())), preferred_element_...  9.24 us
    dot_general x6, matrix products, dot(): return jnp.dot(left, right, preferred_element_type=f32)  6.25 us
    dot_general x4, matrix products, contract_first(): lax.dot_general(left, right, (((0,), (0,)), ((), ())), preferred_element_...  5.33 us

profile of v2, /device:TPU:0, one launch (start us, length us, event | category | flops | bytes accessed | tf_op | source)
XLA Modules:
  0.0 198.3 jit_solution(17301103993843523532)
XLA Ops:
  1.5 1.6 fusion.23
  5.9 1.3 constant_dynamic-slice_fusion.gain
  7.2 35.3 %shard_map.111 = (bf16[4,64,1024]{2,1,0:T(8,128)(2,1)}, bf16[2,4,256,512]{3,2,1,0:T(8,128)(2,1)}, bf16[2,4,4,32,1024]{4,3,2,1,0:T(8,128)(2,1)}, f32[2,1,1024]{2,1,0:T(1,128)}) custom-call(bf16[4,64,1024]{2,1,0:T(8,128)(2,1)} %bitcast.81, bf16[4,32,1024]{2,1,0:T(8,128)(2,1)} %bitcast.87, bf16[256,512]{1,0:T(8,128)(2,1)} %bitcast.100, ...), custom_call_target="tpu_custom_call" | custom-call | tf_op jit(solution)/shard_map/pallas_call | solution.py:299
  42.5 2.8 %fusion.28 = (bf16[1,4,256,512]{3,2,1,0:T(8,128)(2,1)S(1)}, bf16[1,4,256,512]{3,2,1,0:T(8,128)(2,1)}) fusion(bf16[2,4,256,512]{3,2,1,0:T(8,128)(2,1)} %get-tuple-element.26), kind=kLoop, calls=%fused_computation.62 | loop fusion | bytes 4194304 | tf_op jit(solution)/shard_map/slice | solution.py:372
  47.2 17.8 %shard_map.112 = (f32[64,512]{1,0:T(8,128)}, bf16[4,64,512]{2,1,0:T(8,128)(2,1)}, f32[4,1,64]{2,1,0:T(1,128)}, f32[64,1]{1,0:T(8,128)}) custom-call(bf16[4,64,512]{2,1,0:T(8,128)(2,1)} %bitcast.84, f32[64,1]{1,0:T(8,128)} %copy.18.stat), custom_call_target="tpu_custom_call" | custom-call | tf_op jit(solution)/shard_map/pallas_call | solution.py:299
  65.1 2.8 %fusion.27 = (bf16[1,4,4,32,1024]{4,3,2,1,0:T(8,128)(2,1)}, bf16[1,4,4,32,1024]{4,3,2,1,0:T(8,128)(2,1)S(1)}) fusion(bf16[2,4,4,32,1024]{4,3,2,1,0:T(8,128)(2,1)} %get-tuple-element.29), kind=kLoop, calls=%fused_computation.61 | loop fusion | bytes 4194304 | tf_op jit(solution)/shard_map/slice | solution.py:395
  68.4 1.2 copy-done.9
  69.7 1.2 convolution_convert_fusion.6
  71.5 15.9 %shard_map.113 = (f32[64,512]{1,0:T(8,128)}, bf16[4,64,512]{2,1,0:T(8,128)(2,1)}, f32[4,1,64]{2,1,0:T(1,128)}, f32[64,1]{1,0:T(8,128)}) custom-call(bf16[4,64,512]{2,1,0:T(8,128)(2,1)} %bitcast.99, f32[4,1,64]{2,1,0:T(1,128)} %reshape.111.stat), custom_call_target="tpu_custom_call" | custom-call | tf_op jit(solution)/shard_map/pallas_call | solution.py:299
  87.4 2.8 %fusion.6 = f32[256,256]{1,0:T(8,128)} fusion(bf16[256,512]{1,0:T(8,128)(2,1)} %bitcast.95, bf16[512,1024]{1,0:T(8,128)(2,1)} %bitcast.76, bf16[256,1024]{1,0:T(8,128)(2,1)} %copy-done.24, bf16[256,4096]{1,0:T(8,128)(2,1)S(1)} %copy-done, s32[]{:T(128)S(6)} %select_n.16), kind=kOutput, calls=%fused_computation.21 | convolution fusion | flops 403439616 | bytes 2621444 | tf_op jit(solution)/shard_map/dot_general | solution.py:19
  91.0 16.7 %shard_map.114 = (bf16[4,64,256]{2,1,0:T(8,128)(2,1)}, f32[1,128]{1,0:T(1,128)}) custom-call(f32[4,64,256]{2,1,0:T(8,128)} %bitcast.98, s32[64,20]{1,0:T(8,128)} %copy-done.12, s32[64,1]{1,0:T(8,128)} %copy.19.marks), custom_call_target="tpu_custom_call" | custom-call | tf_op jit(solution)/shard_map/pallas_call | solution.py:299
  107.7 1.2 convolution_convert_fusion.3
  109.8 2.4 %convolution_convert_fusion.5 = bf16[256,512]{1,0:T(8,128)(2,1)} fusion(bf16[256,1024]{1,0:T(8,128)(2,1)S(1)} %convolution_convert_fusion.3, bf16[512,1024]{1,0:T(8,128)(2,1)} %bitcast.77), kind=kOutput, calls=%fused_computation.23 | convolution fusion | flops 268566528 | bytes 1835008 | tf_op jit(solution)/shard_map/dot_general | solution.py:19
  112.2 17.6 %shard_map.115 = (bf16[4,64,512]{2,1,0:T(8,128)(2,1)}, f32[4,1,64]{2,1,0:T(1,128)}) custom-call(bf16[4,64,512]{2,1,0:T(8,128)(2,1)} %bitcast.85, f32[64,512]{1,0:T(8,128)} %get-tuple-element.32.upper, f32[64,1]{1,0:T(8,128)} %get-tuple-element.33.recip), custom_call_target="tpu_custom_call" | custom-call | tf_op jit(solution)/shard_map/pallas_call | solution.py:299
  131.0 2.7 %convolution_convert_fusion.2 = bf16[1024,512]{1,0:T(8,128)(2,1)} fusion(bf16[256,512]{1,0:T(8,128)(2,1)} %bitcast.113, bf16[256,1024]{1,0:T(8,128)(2,1)} %copy-done.24, f32[256]{0:T(256)S(1)} %mul.123, f32[1024]{0:T(1024)S(1)} %bitcast.107), kind=kOutput, calls=%fused_computation.12 | convolution fusion | flops 270008320 | bytes 1840128 | tf_op jit(solution)/shard_map/dot_general | solution.py:23
  133.7 1.3 reduce.13
  135.1 2.3 %fusion.8 = (f32[1024]{0:T(1024)S(1)}, bf16[256,1024]{1,0:T(8,128)(2,1)S(1)}) fusion(bf16[256,1024]{1,0:T(8,128)(2,1)} %copy-done.24, f32[256]{0:T(256)S(1)} %mul.123, f32[256]{0:T(256)S(1)} %mul.126, f32[1024]{0:T(1024)S(1)} %bitcast.108, bf16[256,1024]{1,0:T(8,128)(2,1)} %copy-done.1, bf16[256,512]{1,0:T(8,128)(2,1)} %bitcast.114, ...), kind=kOutput, calls=%fused_computation.27 | convolution fusion | flops 271318016 | bytes 2893824 | tf_op jit(solution)/shard_map/dot_general | solution.py:19
  137.5 1.2 convolution_convert_fusion.4
  138.7 15.5 %shard_map.116 = (bf16[4,64,512]{2,1,0:T(8,128)(2,1)}, f32[4,1,64]{2,1,0:T(1,128)}) custom-call(bf16[4,64,512]{2,1,0:T(8,128)(2,1)} %bitcast.86, f32[64,512]{1,0:T(8,128)} %get-tuple-element.37.upper, f32[64,1]{1,0:T(8,128)} %get-tuple-element.38.recip), custom_call_target="tpu_custom_call" | custom-call | tf_op jit(solution)/shard_map/pallas_call | solution.py:299
  154.2 1.7 bitcast_convert_fusion
  156.0 1.5 pad_maximum_fusion.up
  158.5 1.5 pad_maximum_fusion.1.down
  160.7 1.2 bitcast_multiply_fusion
  163.1 30.6 %shard_map.117 = (f32[256,512]{1,0:T(8,128)}, bf16[4,32,1024]{2,1,0:T(8,128)(2,1)}, f32[4,1,1152]{2,1,0:T(1,128)}) custom-call(bf16[2,4,256,512]{3,2,1,0:T(8,128)(2,1)} %pad_maximum_fusion.up, bf16[2,4,4,32,1024]{4,3,2,1,0:T(8,128)(2,1)} %pad_maximum_fusion.1.down, f32[2,1,1152]{2,1,0:T(1,128)} %pad_maximum_fusion.2.small), custom_call_target="tpu_custom_call" | custom-call | tf_op jit(solution)/shard_map/pallas_call | solution.py:299
  (84 shorter events, 17.1 us)
Async XLA Ops:
  0.6 2.8 %copy-start = (bf16[256,4096]{1,0:T(8,128)(2,1)S(1)}, bf16[256,4096]{1,0:T(8,128)(2,1)}, u32[]{:S(2)}) copy-start(bf16[256,4096]{1,0:T(8,128)(2,1)} %param.12) | copy-start | bytes 6291460
  0.6 2.5 %copy-start.18 = (s32[128,20]{0,1:T(8,128)S(1)}, s32[128,20]{0,1:T(8,128)}, u32[]{:S(2)}) copy-start(s32[128,20]{0,1:T(8,128)} %param.10) | copy-start | bytes 30724
  3.3 1.6 copy-start.12
  3.4 1.5 copy-start.16
  42.4 2.8 %copy-start.19 = (f32[2,1,1024]{2,1,0:T(1,128)S(1)}, f32[2,1,1024]{2,1,0:T(1,128)}, u32[]{:S(2)}) copy-start(f32[2,1,1024]{2,1,0:T(1,128)} %get-tuple-element.25) | copy-start | bytes 24580
  42.5 2.8 %copy-start.7 = (bf16[4,64,1024]{2,1,0:T(8,128)(2,1)S(1)}, bf16[4,64,1024]{2,1,0:T(8,128)(2,1)}, u32[]{:S(2)}) copy-start(bf16[4,64,1024]{2,1,0:T(8,128)(2,1)} %get-tuple-element.24) | copy-start | bytes 1572868
  65.0 2.8 %copy-start.8 = (bf16[4,64,1024]{2,1,0:T(8,128)(2,1)S(1)}, bf16[4,64,1024]{2,1,0:T(8,128)(2,1)}, u32[]{:S(2)}) copy-start(bf16[4,64,1024]{2,1,0:T(8,128)(2,1)} %get-tuple-element.24) | copy-start | bytes 1572868
  65.1 2.8 %copy-start.13 = (bf16[4,64,512]{2,1,0:T(8,128)(2,1)S(1)}, bf16[4,64,512]{2,1,0:T(8,128)(2,1)}, u32[]{:S(2)}) copy-start(bf16[4,64,512]{2,1,0:T(8,128)(2,1)} %get-tuple-element.28) | copy-start | bytes 786436
  67.9 3.0 %copy-start.3 = (bf16[1,4,4,32,1024]{4,3,2,1,0:T(8,128)(2,1)}, bf16[1,4,4,32,1024]{4,3,2,1,0:T(8,128)(2,1)S(1)}, u32[]{:S(2)}) copy-start(bf16[1,4,4,32,1024]{4,3,2,1,0:T(8,128)(2,1)S(1)} %get-tuple-element.45) | copy-start | bytes 3145732
  67.9 1.8 copy-start.9
  68.4 2.4 %copy-start.24 = (bf16[256,1024]{1,0:T(8,128)(2,1)}, bf16[256,1024]{1,0:T(8,128)(2,1)S(1)}, u32[]{:S(2)}) copy-start(bf16[256,1024]{1,0:T(8,128)(2,1)S(1)} %get-tuple-element.55) | copy-start | bytes 1572868
  69.7 20.6 %copy-start.23 = (s32[128]{0:T(128)S(1)}, s32[128]{0:T(128)}, u32[]{:S(2)}) copy-start(s32[128]{0:T(128)} %param.11) | copy-start | bytes 1540
  90.3 40.0 %copy-start.21 = (f32[4,1,64]{2,1,0:T(1,128)S(1)}, f32[4,1,64]{2,1,0:T(1,128)}, u32[]{:S(2)}) copy-start(f32[4,1,64]{2,1,0:T(1,128)} %get-tuple-element.35) | copy-start | bytes 3076
  135.1 2.3 %copy-start.4 = (bf16[1,4,4,32,1024]{4,3,2,1,0:T(8,128)(2,1)S(1)}, bf16[1,4,4,32,1024]{4,3,2,1,0:T(8,128)(2,1)}, u32[]{:S(2)}) copy-start(bf16[1,4,4,32,1024]{4,3,2,1,0:T(8,128)(2,1)} %copy-done.3) | copy-start | bytes 3145732
  137.4 1.2 copy-start.5
  137.4 16.8 %copy-start.20 = (f32[4,1,64]{2,1,0:T(1,128)S(1)}, f32[4,1,64]{2,1,0:T(1,128)}, u32[]{:S(2)}) copy-start(f32[4,1,64]{2,1,0:T(1,128)} %get-tuple-element.27) | copy-start | bytes 3076
  154.2 1.8 copy-start.10
  156.0 1.5 copy-start.2
  156.0 1.5 copy-start.14
  156.0 2.0 %copy-start.6 = (bf16[256,1024]{1,0:T(8,128)(2,1)S(1)}, bf16[256,1024]{1,0:T(8,128)(2,1)}, u32[]{:S(2)}) copy-start(bf16[256,1024]{1,0:T(8,128)(2,1)} %copy-done.5) | copy-start | bytes 1572868
  158.5 3.4 %copy-start.15 = (bf16[4,64,512]{2,1,0:T(8,128)(2,1)S(1)}, bf16[4,64,512]{2,1,0:T(8,128)(2,1)}, u32[]{:S(2)}) copy-start(bf16[4,64,512]{2,1,0:T(8,128)(2,1)} %get-tuple-element.39) | copy-start | bytes 786436
  160.0 2.5 %copy-start.22 = (f32[1,128]{1,0:T(1,128)S(1)}, f32[1,128]{1,0:T(1,128)}, u32[]{:S(2)}) copy-start(f32[1,128]{1,0:T(1,128)} %get-tuple-element.40) | copy-start | bytes 1540
  193.7 2.6 %copy-start.17 = (f32[4,1,1152]{2,1,0:T(1,128)S(1)}, f32[4,1,1152]{2,1,0:T(1,128)}, u32[]{:S(2)}) copy-start(f32[4,1,1152]{2,1,0:T(1,128)} %get-tuple-element.43) | copy-start | bytes 55300
  193.7 3.8 %copy-start.11 = (f32[256,512]{1,0:T(8,128)S(1)}, f32[256,512]{1,0:T(8,128)}, u32[]{:S(2)}) copy-start(f32[256,512]{1,0:T(8,128)} %get-tuple-element.41) | copy-start | bytes 1572868
  (1 other events, 0.8 us)
